TPU v7x, 32 devices: a whole 2x2x4 slice. The times are simulated.
32 devices in a mesh: seq: 16 (over z, y, x), chan: 2 (over core).
Axes of the slice: x: 2, y: 2, z: 4, core: 2. Of those that a mesh axis runs over, the one named last changes fastest.
Arguments:
- tokens: float32 [2048, 1024], P('seq', 'chan'), may hold values from -6 to 6
- gate_weight: float32 [1024, 1024], P(None, 'chan'), may hold values from -0.1875 to 0.1875
- value_weight: float32 [1024, 1024], P(None, 'chan'), may hold values from -0.1875 to 0.1875
- output_weight: float32 [1024, 1024], P('chan'), may hold values from -0.1875 to 0.1875
- wave_numbers: int32 [32], replicated, may hold values from 1 to 2047
- position_in: float32 [64, 64], replicated, may hold values from -0.75 to 0.75
- bias_in: float32 [64], replicated, may hold values from -3 to 3
- position_mid: float32 [64, 64], replicated, may hold values from -0.75 to 0.75
- bias_mid: float32 [64], replicated, may hold values from -3 to 3
- position_out: float32 [64, 1024], P(None, 'chan'), may hold values from -1 to 1
- decay_rate: float32 [1024], P('chan'), may hold values from 0.5 to 51.2
Outputs:
- mixed_tokens: float32 [2048, 1024], P('seq', 'chan')
All inputs are finite; a program needn't handle non-finite values.
Results may differ from a plain program's by a relative error of at most 0.0003.
Values sent between devices are 32-bit elements; how exact they have to be, the bound alone decides.
A program may use at most 64 MiB of HBM per device.

v0:
```python
import functools
import math

import jax
import jax.numpy as jnp
import numpy as np
from jax import lax
from jax.experimental import pallas as pl
from jax.experimental.pallas import tpu as pltpu
from jax.sharding import PartitionSpec as P

PERIOD = 4096
GROUPS = 2
F32 = jnp.float32
BF16 = jnp.bfloat16
MESH = pl.DeviceIdType.MESH


def split(a):
    hi = a.astype(BF16)
    return hi, (a - hi.astype(F32)).astype(BF16)


def mm(a, b, dims=((1,), (0,))):
    return lax.dot_general(a, b, (dims, ((), ())), preferred_element_type=F32)


def dot3(a, b, dims=((1,), (0,))):
    (ah, al), (bh, bl) = a, b
    return mm(ah, bh, dims) + (mm(ah, bl, dims) + mm(al, bh, dims))


def silu(v):
    return v / (1.0 + jnp.exp(-v))


def cmul_const(z, angle):
    c, s = math.cos(angle), math.sin(angle)
    re, im = z
    if abs(s) < 1e-12:
        return (re, im) if c > 0 else (-re, -im)
    if abs(c) < 1e-12:
        return (-im, re) if s > 0 else (im, -re)
    return (re * c - im * s, re * s + im * c)


def fft(xs, sign):
    n = len(xs)
    if n == 1:
        return xs
    even, odd = fft(xs[0::2], sign), fft(xs[1::2], sign)
    low, high = [], []
    for k in range(n // 2):
        er, ei = even[k]
        tr, ti = cmul_const(odd[k], sign * 2.0 * math.pi * k / n)
        low.append((er + tr, ei + ti))
        high.append((er - tr, ei - ti))
    return low + high


def tables(outer, inner):
    length = outer * inner
    r = np.arange(inner)
    turn = 2.0 * np.pi * np.outer(np.arange(outer) + 0.25, r) / length
    turns = np.concatenate([np.cos(turn), np.sin(turn)], 0).astype(np.float32)
    ang = 2.0 * np.pi * (np.outer(r, r) % inner) / inner
    c, s = np.cos(ang), np.sin(ang)
    fwd = np.block([[c, -s], [s, c]]).astype(np.float32)
    inv = (np.block([[c, s], [-s, c]]) / length).astype(np.float32)

    def halves(a):
        hi = a.astype(jnp.bfloat16)
        return [hi, (a - hi.astype(np.float32)).astype(jnp.bfloat16)]

    return turns, np.stack(halves(fwd) + halves(inv))


def column(row, first, count):
    n = row.shape[1]
    i = lax.broadcasted_iota(jnp.int32, (count, n), 0)
    j = lax.broadcasted_iota(jnp.int32, (count, n), 1)
    picked = jnp.where(j == i + first, jnp.broadcast_to(row, (count, n)), jnp.zeros_like(row))
    return jnp.sum(picked, axis=1, keepdims=True)


def forward(blocks, turn_ref, mat_ref):
    outer = len(blocks)
    step = -2.0 * math.pi / (4 * outer)
    twisted = [(b * math.cos(step * s), b * math.sin(step * s)) if s else (b, None) for s, b in enumerate(blocks)]
    twisted[0] = (blocks[0], jnp.zeros_like(blocks[0]))
    rows = []
    for k, (re, im) in enumerate(fft(twisted, -1.0)):
        c, s = turn_ref[k : k + 1, :], turn_ref[outer + k : outer + k + 1, :]
        rows.append(jnp.concatenate([re * c + im * s, im * c - re * s], axis=1))
    grid = jnp.concatenate(rows, axis=0)
    return dot3(split(grid), (mat_ref[0], mat_ref[1]))


def backward(spectrum, outer, turn_ref, mat_ref):
    back = dot3(split(spectrum), (mat_ref[2], mat_ref[3]))
    chans, inner = spectrum.shape[0] // outer, spectrum.shape[1] // 2
    zs = []
    for k in range(outer):
        re = back[k * chans : (k + 1) * chans, :inner]
        im = back[k * chans : (k + 1) * chans, inner:]
        c, s = turn_ref[k : k + 1, :], turn_ref[outer + k : outer + k + 1, :]
        zs.append((re * c - im * s, re * s + im * c))
    ys = fft(zs, 1.0)
    step = 2.0 * math.pi / (4 * outer)
    return [re * math.cos(step * s) - im * math.sin(step * s) for s, (re, im) in enumerate(ys)]


def position_blocks(outer, inner, chans, first, wave, w_in, b_in, w_mid, b_mid, w_out, decay):
    length = outer * inner
    waves = wave.shape[1]
    hid = w_in.shape[1]
    wcol = column(wave[...], 0, waves)
    unit = 2.0 * math.pi / PERIOD

    def trig(spots):
        ang = (lax.rem(spots * wcol, PERIOD)).astype(F32) * unit
        return jnp.cos(ang), jnp.sin(ang)

    rc, rs = trig(lax.broadcasted_iota(jnp.int32, (waves, inner), 1))
    sc, ss = trig(lax.broadcasted_iota(jnp.int32, (waves, max(outer, 128)), 1) * inner)
    bi, bm = column(b_in[...], 0, hid), column(b_mid[...], 0, w_mid.shape[1])
    wi, wm = split(w_in[...].T), split(w_mid[...].T)
    width = w_out.shape[1]
    i = lax.broadcasted_iota(jnp.int32, (chans, width), 0)
    j = lax.broadcasted_iota(jnp.int32, (chans, width), 1)
    pick = jnp.where(j == i + first, 1.0, 0.0).astype(BF16)
    oh, ol = split(w_out[...])
    nt = ((1,), (1,))
    own = (mm(pick, oh, nt).astype(BF16), mm(pick, ol, nt).astype(BF16))
    dec = column(decay[...], first, chans)
    gain = jnp.sqrt(2.0 * dec / length)
    per = max(1, 2048 // inner)
    blocks = []
    for s0 in range(0, outer, per):
        some = range(s0, min(outer, s0 + per))
        cs, sn = [], []
        for s in some:
            a, b = sc[:, s : s + 1], ss[:, s : s + 1]
            cs.append(rc * a - rs * b)
            sn.append(rs * a + rc * b)
        feats = jnp.concatenate([jnp.concatenate(cs, 1), jnp.concatenate(sn, 1)], 0)
        h = jnp.maximum(dot3(wi, split(feats)) + bi, 0.0)
        h = jnp.maximum(dot3(wm, split(h)) + bm, 0.0)
        shape = dot3(own, split(h))
        n = (lax.broadcasted_iota(jnp.int32, shape.shape, 1) + s0 * inner).astype(F32) / length
        kern = shape * (jnp.exp(-dec * n) * gain)
        blocks += [kern[:, q * inner : (q + 1) * inner] for q in range(len(some))]
    return blocks


def body(
    n, m, groups,
    tok_hbm, gate_hbm, value_hbm, out_hbm, turn_hbm, mat_hbm,
    wave_hbm, w_in_hbm, b_in_hbm, w_mid_hbm, b_mid_hbm, w_out_hbm, decay_hbm,
    result,
    wave, w_in, b_in, w_mid, b_mid, w_out, decay,
    tok, gate_w, value_w, out_w, turn, mat, sent, got, conv_out, conv_in, part_out, part_in,
    load_sem, up_sem, all_sem, tok_send, tok_recv, a_send, a_recv, b_send, b_recv, p_send, p_recv,
):
    me, mine = lax.axis_index("seq"), lax.axis_index("chan")
    rows, depth = tok_hbm.shape
    width = value_w.shape[1]
    chans = width // n
    per = chans // groups
    farthest = range(n - 1, 0, -1)

    def partner(i):
        if n & (n - 1):
            return lax.rem(me + i, n)
        bit, to = 1, 0
        while bit < n:
            here = lax.rem(me // bit, 2)
            to = to + (1 - here if i & bit else here) * bit
            bit *= 2
        return to


    barrier = pltpu.get_barrier_semaphore()
    for i in farthest:
        pl.semaphore_signal(barrier, inc=1, device_id={"seq": partner(i), "chan": 0}, device_id_type=MESH)

    @pl.when(mine == 0)
    def _():
        pl.semaphore_signal(barrier, inc=1, device_id={"chan": 1}, device_id_type=MESH)

    loads = [
        pltpu.make_async_copy(src, dst, load_sem.at[i])
        for i, (src, dst) in enumerate(
            [
                (tok_hbm, tok.at[mine]), (value_hbm, value_w), (gate_hbm, gate_w), (mat_hbm, mat), (turn_hbm, turn), (out_hbm, out_w),
                (wave_hbm, wave), (w_in_hbm, w_in), (b_in_hbm, b_in), (w_mid_hbm, w_mid), (b_mid_hbm, b_mid), (w_out_hbm, w_out), (decay_hbm, decay),
            ]
        )
    ]
    for c in loads:
        c.start()

    def project(who, w_ref):
        lines = pl.ds(pl.multiple_of(who * depth, 8), depth)
        return dot3(split(tok[who]), split(w_ref[lines, :]))

    loads[0].wait()

    @pl.when(mine == 1)
    def _():
        pl.semaphore_wait(barrier, 1)
        pl.semaphore_signal(up_sem, inc=1, device_id={"chan": 0}, device_id_type=MESH)

    @pl.when(mine == 0)
    def _():
        pl.semaphore_wait(up_sem, 1)

    tok_copies = []
    for i in range(1, m):
        c = pltpu.make_async_remote_copy(
            src_ref=tok.at[mine], dst_ref=tok.at[mine], send_sem=tok_send.at[i], recv_sem=tok_recv.at[i],
            device_id={"chan": lax.rem(mine + i, m)}, device_id_type=MESH,
        )
        c.start()
        tok_copies.append(c)
    loads[1].wait()
    value_sum = project(mine, value_w)
    for i in range(1, m):
        tok_copies[i - 1].wait_recv()
        value_sum = value_sum + project(lax.rem(mine + m - i, m), value_w)
    sent[...] = silu(value_sum).T

    @pl.when(mine == 0)
    def _():
        pl.semaphore_wait(barrier, 2 * (n - 1))
        pl.semaphore_signal(all_sem, inc=1, device_id={"chan": 1}, device_id_type=MESH)

    @pl.when(mine == 1)
    def _():
        pl.semaphore_wait(all_sem, 1)

    a_copies = {}
    for g in range(groups):
        for i in farthest:
            to = partner(i)
            c = pltpu.make_async_remote_copy(
                src_ref=sent.at[pl.ds(pl.multiple_of(to * chans + g * per, 8), per), :],
                dst_ref=got.at[me, pl.ds(g * per, per), :],
                send_sem=a_send.at[g * n + i], recv_sem=a_recv.at[g * n + i],
                device_id={"seq": to}, device_id_type=MESH,
            )
            c.start()
            a_copies[g, i] = c
    got[me] = sent[pl.ds(pl.multiple_of(me * chans, 8), chans), :]

    for c in loads[3:5] + loads[6:]:
        c.wait()
    kernel_blocks = position_blocks(n, rows, chans, me * chans, wave, w_in, b_in, w_mid, b_mid, w_out, decay)
    kernel_specs = []
    for g in range(groups):
        kernel_specs.append(forward([b[g * per : (g + 1) * per] for b in kernel_blocks], turn, mat))

    b_copies = {}
    for g in range(groups):
        for i in range(1, n):
            a_copies[g, i].wait_recv()
        spec = forward([got[s, g * per : (g + 1) * per, :] for s in range(n)], turn, mat)
        vr, vi = spec[:, :rows], spec[:, rows:]
        kr, ki = kernel_specs[g][:, :rows], kernel_specs[g][:, rows:]
        prod = jnp.concatenate([vr * kr - vi * ki, vr * ki + vi * kr], axis=1)
        for s, y in enumerate(backward(prod, n, turn, mat)):
            conv_out[s, g * per : (g + 1) * per, :] = y
        for i in farthest:
            to = partner(i)
            c = pltpu.make_async_remote_copy(
                src_ref=conv_out.at[to, pl.ds(g * per, per), :],
                dst_ref=conv_in.at[me, pl.ds(g * per, per), :],
                send_sem=b_send.at[g * n + i], recv_sem=b_recv.at[g * n + i],
                device_id={"seq": to}, device_id_type=MESH,
            )
            c.start()
            b_copies[g, i] = c
        conv_in[me, g * per : (g + 1) * per, :] = conv_out[me, g * per : (g + 1) * per, :]

    loads[2].wait()
    gate_sum = project(mine, gate_w)
    for i in range(1, m):
        gate_sum = gate_sum + project(lax.rem(mine + m - i, m), gate_w)
    gated = silu(gate_sum)
    loads[5].wait()
    gate_lines = gated.T.reshape(n, chans, rows)

    def partial(mixed, g, who):
        cols = pl.ds(pl.multiple_of(who * depth, 128), depth)
        lines = out_w[:, cols].reshape(n, chans, depth)[:, g * per : (g + 1) * per, :]
        return dot3(mixed, split(lines.reshape(n * per, depth)))

    sums = [0.0] * m
    for g in range(groups):
        some = slice(g * per, (g + 1) * per)
        for i in farthest:
            b_copies[g, i].wait_recv()
        mixed = split((gate_lines[:, some, :] * conv_in[:, some, :]).reshape(n * per, rows).T)
        if g < groups - 1:
            sums = [t + partial(mixed, g, lax.rem(mine + i, m)) for i, t in enumerate(sums)]

    p_copies = []
    for i in range(1, m):
        to = lax.rem(mine + i, m)
        part_out[i - 1] = sums[i] + partial(mixed, groups - 1, to)
        c = pltpu.make_async_remote_copy(
            src_ref=part_out.at[i - 1], dst_ref=part_in.at[i - 1], send_sem=p_send.at[i], recv_sem=p_recv.at[i],
            device_id={"chan": to}, device_id_type=MESH,
        )
        c.start()
        p_copies.append(c)
    total = sums[0] + partial(mixed, groups - 1, mine)
    for i in range(1, m):
        p_copies[i - 1].wait_recv()
        total = total + part_in[i - 1]
    result[...] = total
    for c in tok_copies + list(a_copies.values()) + list(b_copies.values()) + p_copies:
        c.wait_send()


def on_device(
    tokens, gate_weight, value_weight, output_weight, wave_numbers,
    position_in, bias_in, position_mid, bias_mid, position_out, decay_rate,
):
    n, m = lax.axis_size("seq"), lax.axis_size("chan")
    rows, depth = tokens.shape
    width = gate_weight.shape[1]
    chans = width // n
    groups = max(1, min(GROUPS, chans // 8))
    assert m == 2
    turns, mats = tables(n, rows)
    hbm = pl.BlockSpec(memory_space=pl.ANY)
    vmem = pl.BlockSpec(memory_space=pltpu.VMEM)
    dma = pltpu.SemaphoreType.DMA
    return pl.pallas_call(
        functools.partial(body, n, m, groups),
        out_shape=pltpu.VMEM((rows, depth), F32),
        in_specs=[hbm] * 13,
        out_specs=vmem,
        scratch_shapes=[
            pltpu.VMEM((1, wave_numbers.shape[0]), jnp.int32),
            pltpu.VMEM(position_in.shape, F32),
            pltpu.VMEM((1, bias_in.shape[0]), F32),
            pltpu.VMEM(position_mid.shape, F32),
            pltpu.VMEM((1, bias_mid.shape[0]), F32),
            pltpu.VMEM(position_out.shape, F32),
            pltpu.VMEM((1, width), F32),
            pltpu.VMEM((m, rows, depth), F32),
            pltpu.VMEM(gate_weight.shape, F32),
            pltpu.VMEM(value_weight.shape, F32),
            pltpu.VMEM(output_weight.shape, F32),
            pltpu.VMEM(turns.shape, F32),
            pltpu.VMEM(mats.shape, BF16),
            pltpu.VMEM((width, rows), F32),
            pltpu.VMEM((n, chans, rows), F32),
            pltpu.VMEM((n, chans, rows), F32),
            pltpu.VMEM((n, chans, rows), F32),
            pltpu.VMEM((max(1, m - 1), rows, depth), F32),
            pltpu.VMEM((max(1, m - 1), rows, depth), F32),
            dma((13,)),
            pltpu.SemaphoreType.REGULAR,
            pltpu.SemaphoreType.REGULAR,
            dma((m,)), dma((m,)),
            dma((groups * n,)), dma((groups * n,)),
            dma((groups * n,)), dma((groups * n,)),
            dma((m,)), dma((m,)),
        ],
        compiler_params=pltpu.CompilerParams(collective_id=0, has_side_effects=True),
    )(
        tokens, gate_weight, value_weight, output_weight, jnp.asarray(turns), jnp.asarray(mats),
        wave_numbers[None, :], position_in, bias_in[None, :], position_mid, bias_mid[None, :],
        position_out, decay_rate[None, :],
    )


def solution(mesh):
    placed = (
        P("seq", "chan"), P(None, "chan"), P(None, "chan"), P("chan", None),
        P(), P(), P(), P(), P(), P(None, "chan"), P("chan"),
    )
    return jax.shard_map(
        on_device, mesh=mesh, in_specs=placed, out_specs=P("seq", "chan"), check_vma=False
    )
```

profile of v0, /device:TPU:0, one launch (start us, length us, event | category | flops | bytes accessed | tf_op | source)
XLA Modules:
  0.0 24.3 jit_solution(13719230432339391376)
XLA Ops:
  0.0 23.5 %shard_map.127 = f32[128,512]{1,0:T(8,128)S(1)} custom-call(f32[128,512]{1,0:T(8,128)} %tok_hbm.1, f32[1024,512]{1,0:T(8,128)} %gate_hbm.1, f32[1024,512]{1,0:T(8,128)} %value_hbm.1, f32[512,1024]{1,0:T(8,128)} %out_hbm.1, f32[32,128]{1,0:T(8,128)} %constant.4.clone.turn_hbm, bf16[4,256,256]{2,1,0:T(8,128)(2,1)} %constant.5.clone.mat_hbm, s32[1,32]{1,0:T(1,128)} %bitcast.5, ...), custom_call_target="tpu_custom_call" | custom-call | tf_op jit(solution)/shard_map/pallas_call | solution.py:340
  23.6 0.7 %copy.15 = f32[128,512]{1,0:T(8,128)} copy(f32[128,512]{1,0:T(8,128)S(1)} %shard_map.127) | data formatting | bytes 524288
where the time goes:
time: 24.4 us; the launch traced here: 24.3 us
  Pallas kernels  23.5 us (96%)
  local copies, waits for them, and re-layouts  0.71 us (3%)
    pallas_call x1, Pallas kernels, on_device(): pl.pallas_call(functools.partial(body, n, m, groups), out_shape=pltpu.VME...  23.5 us
    unnamed x1, local copies, waits for them, and re-layouts  0.71 us

commit v1 on v0

--- a/solution.py
+++ b/solution.py
@@ -200,6 +200,10 @@
     for c in loads:
         c.start()
 
+    def arrived(ref, g, sem):
+        block = ref.at[pl.ds(0, n - 1), pl.ds(g * per, per), :]
+        pltpu.make_async_copy(block, block, sem).wait()
+
     def project(who, w_ref):
         lines = pl.ds(pl.multiple_of(who * depth, 8), depth)
         return dot3(split(tok[who]), split(w_ref[lines, :]))
@@ -239,18 +243,16 @@
     def _():
         pl.semaphore_wait(all_sem, 1)
 
-    a_copies = {}
     for g in range(groups):
         for i in farthest:
             to = partner(i)
             c = pltpu.make_async_remote_copy(
                 src_ref=sent.at[pl.ds(pl.multiple_of(to * chans + g * per, 8), per), :],
                 dst_ref=got.at[me, pl.ds(g * per, per), :],
-                send_sem=a_send.at[g * n + i], recv_sem=a_recv.at[g * n + i],
+                send_sem=a_send, recv_sem=a_recv.at[g],
                 device_id={"seq": to}, device_id_type=MESH,
             )
             c.start()
-            a_copies[g, i] = c
     got[me] = sent[pl.ds(pl.multiple_of(me * chans, 8), chans), :]
 
     for c in loads[3:5] + loads[6:]:
@@ -260,10 +262,8 @@
     for g in range(groups):
         kernel_specs.append(forward([b[g * per : (g + 1) * per] for b in kernel_blocks], turn, mat))
 
-    b_copies = {}
-    for g in range(groups):
-        for i in range(1, n):
-            a_copies[g, i].wait_recv()
+    for g in range(groups):
+        arrived(got, g, a_recv.at[g])
         spec = forward([got[s, g * per : (g + 1) * per, :] for s in range(n)], turn, mat)
         vr, vi = spec[:, :rows], spec[:, rows:]
         kr, ki = kernel_specs[g][:, :rows], kernel_specs[g][:, rows:]
@@ -275,11 +275,10 @@
             c = pltpu.make_async_remote_copy(
                 src_ref=conv_out.at[to, pl.ds(g * per, per), :],
                 dst_ref=conv_in.at[me, pl.ds(g * per, per), :],
-                send_sem=b_send.at[g * n + i], recv_sem=b_recv.at[g * n + i],
+                send_sem=b_send, recv_sem=b_recv.at[g],
                 device_id={"seq": to}, device_id_type=MESH,
             )
             c.start()
-            b_copies[g, i] = c
         conv_in[me, g * per : (g + 1) * per, :] = conv_out[me, g * per : (g + 1) * per, :]
 
     loads[2].wait()
@@ -298,8 +297,7 @@
     sums = [0.0] * m
     for g in range(groups):
         some = slice(g * per, (g + 1) * per)
-        for i in farthest:
-            b_copies[g, i].wait_recv()
+        arrived(conv_in, g, b_recv.at[g])
         mixed = split((gate_lines[:, some, :] * conv_in[:, some, :]).reshape(n * per, rows).T)
         if g < groups - 1:
             sums = [t + partial(mixed, g, lax.rem(mine + i, m)) for i, t in enumerate(sums)]
@@ -319,7 +317,10 @@
         p_copies[i - 1].wait_recv()
         total = total + part_in[i - 1]
     result[...] = total
-    for c in tok_copies + list(a_copies.values()) + list(b_copies.values()) + p_copies:
+    for g in range(groups):
+        arrived(got, g, a_send)
+        arrived(conv_in, g, b_send)
+    for c in tok_copies + p_copies:
         c.wait_send()
 
 
@@ -366,8 +367,8 @@
             pltpu.SemaphoreType.REGULAR,
             pltpu.SemaphoreType.REGULAR,
             dma((m,)), dma((m,)),
-            dma((groups * n,)), dma((groups * n,)),
-            dma((groups * n,)), dma((groups * n,)),
+            dma, dma((groups,)),
+            dma, dma((groups,)),
             dma((m,)), dma((m,)),
         ],
         compiler_params=pltpu.CompilerParams(collective_id=0, has_side_effects=True),

time: 24.4 us -> 23.3 us (0.955)
  Pallas kernels: 23.5 us -> 22.4 us
    pallas_call x1, Pallas kernels: 23.5 us -> 22.4 us  [on_device(): pl.pallas_call(functools.partial(body, n, m, groups), out_shape=pltpu.VME...]
where the time goes in v1:
time: 23.3 us; the launch traced here: 23.1 us
  Pallas kernels  22.4 us (96%)
  local copies, waits for them, and re-layouts  0.71 us (3%)
    pallas_call x1, Pallas kernels, on_device(): pl.pallas_call(functools.partial(body, n, m, groups), out_shape=pltpu.VME...  22.4 us
    unnamed x1, local copies, waits for them, and re-layouts  0.71 us

profile of v1, /device:TPU:0, one launch (start us, length us, event | category | flops | bytes accessed | tf_op | source)
XLA Modules:
  0.0 23.1 jit_solution(9368678790341715719)
XLA Ops:
  0.0 22.4 %shard_map.127 = f32[128,512]{1,0:T(8,128)S(1)} custom-call(f32[128,512]{1,0:T(8,128)} %tok_hbm.1, f32[1024,512]{1,0:T(8,128)} %gate_hbm.1, f32[1024,512]{1,0:T(8,128)} %value_hbm.1, f32[512,1024]{1,0:T(8,128)} %out_hbm.1, f32[32,128]{1,0:T(8,128)} %constant.4.clone.turn_hbm, bf16[4,256,256]{2,1,0:T(8,128)(2,1)} %constant.5.clone.mat_hbm, s32[1,32]{1,0:T(1,128)} %bitcast.5, ...), custom_call_target="tpu_custom_call" | custom-call | tf_op jit(solution)/shard_map/pallas_call | solution.py:341
  22.4 0.7 %copy.15 = f32[128,512]{1,0:T(8,128)} copy(f32[128,512]{1,0:T(8,128)S(1)} %shard_map.127) | data formatting | bytes 524288

commit v2 on v1

v2 whole, which is shorter than its diff:
```python
import functools
import math

import jax
import jax.numpy as jnp
import numpy as np
from jax import lax
from jax.experimental import pallas as pl
from jax.experimental.pallas import tpu as pltpu
from jax.sharding import PartitionSpec as P

PERIOD = 4096
F32 = jnp.float32
BF16 = jnp.bfloat16
MESH = pl.DeviceIdType.MESH


def split(a):
    hi = a.astype(BF16)
    return hi, (a - hi.astype(F32)).astype(BF16)


def mm(a, b, dims=((1,), (0,))):
    return lax.dot_general(a, b, (dims, ((), ())), preferred_element_type=F32)


def dot3(a, b, dims=((1,), (0,))):
    (ah, al), (bh, bl) = a, b
    return mm(ah, bh, dims) + (mm(ah, bl, dims) + mm(al, bh, dims))


def silu(v):
    return v / (1.0 + jnp.exp(-v))


def cmul_const(z, angle):
    c, s = math.cos(angle), math.sin(angle)
    re, im = z
    if abs(s) < 1e-12:
        return (re, im) if c > 0 else (-re, -im)
    if abs(c) < 1e-12:
        return (-im, re) if s > 0 else (im, -re)
    return (re * c - im * s, re * s + im * c)


def fft(xs, sign):
    n = len(xs)
    if n == 1:
        return xs
    even, odd = fft(xs[0::2], sign), fft(xs[1::2], sign)
    low, high = [], []
    for k in range(n // 2):
        er, ei = even[k]
        tr, ti = cmul_const(odd[k], sign * 2.0 * math.pi * k / n)
        low.append((er + tr, ei + ti))
        high.append((er - tr, ei - ti))
    return low + high


def tables(outer, inner):
    length = outer * inner
    r = np.arange(inner)
    turn = 2.0 * np.pi * np.outer(np.arange(outer) + 0.25, r) / length
    turns = np.concatenate([np.cos(turn), np.sin(turn)], 0).astype(np.float32)
    ang = 2.0 * np.pi * (np.outer(r, r) % inner) / inner
    c, s = np.cos(ang), np.sin(ang)
    fwd = np.block([[c, -s], [s, c]]).astype(np.float32)
    inv = (np.block([[c, s], [-s, c]]) / length).astype(np.float32)

    def halves(a):
        hi = a.astype(jnp.bfloat16)
        return [hi, (a - hi.astype(np.float32)).astype(jnp.bfloat16)]

    return turns, np.stack(halves(fwd) + halves(inv))


def column(row, first, count):
    n = row.shape[1]
    i = lax.broadcasted_iota(jnp.int32, (count, n), 0)
    j = lax.broadcasted_iota(jnp.int32, (count, n), 1)
    picked = jnp.where(j == i + first, jnp.broadcast_to(row, (count, n)), jnp.zeros_like(row))
    return jnp.sum(picked, axis=1, keepdims=True)


def forward(blocks, turn_ref, mat_ref):
    outer = len(blocks)
    step = -2.0 * math.pi / (4 * outer)
    twisted = [(b * math.cos(step * s), b * math.sin(step * s)) if s else (b, None) for s, b in enumerate(blocks)]
    twisted[0] = (blocks[0], jnp.zeros_like(blocks[0]))
    rows = []
    for k, (re, im) in enumerate(fft(twisted, -1.0)):
        c, s = turn_ref[k : k + 1, :], turn_ref[outer + k : outer + k + 1, :]
        rows.append(jnp.concatenate([re * c + im * s, im * c - re * s], axis=1))
    grid = jnp.concatenate(rows, axis=0)
    return dot3(split(grid), (mat_ref[0], mat_ref[1]))


def backward(spectrum, outer, turn_ref, mat_ref):
    back = dot3(split(spectrum), (mat_ref[2], mat_ref[3]))
    chans, inner = spectrum.shape[0] // outer, spectrum.shape[1] // 2
    zs = []
    for k in range(outer):
        re = back[k * chans : (k + 1) * chans, :inner]
        im = back[k * chans : (k + 1) * chans, inner:]
        c, s = turn_ref[k : k + 1, :], turn_ref[outer + k : outer + k + 1, :]
        zs.append((re * c - im * s, re * s + im * c))
    ys = fft(zs, 1.0)
    step = 2.0 * math.pi / (4 * outer)
    return [re * math.cos(step * s) - im * math.sin(step * s) for s, (re, im) in enumerate(ys)]


def cmul(a, b):
    half = a.shape[1] // 2
    ar, ai, br, bi = a[:, :half], a[:, half:], b[:, :half], b[:, half:]
    return jnp.concatenate([ar * br - ai * bi, ar * bi + ai * br], axis=1)


def position_blocks(length, inner, parts, first, chans, wave, w_in, b_in, w_mid, b_mid, w_out, decay):
    waves = wave.shape[1]
    hid = w_in.shape[1]
    wcol = column(wave[...], 0, waves)
    unit = 2.0 * math.pi / PERIOD

    def trig(spots):
        ang = (lax.rem(spots * wcol, PERIOD)).astype(F32) * unit
        return jnp.cos(ang), jnp.sin(ang)

    rc, rs = trig(lax.broadcasted_iota(jnp.int32, (waves, inner), 1))
    sc, ss = trig(lax.broadcasted_iota(jnp.int32, (waves, max(length // inner, 128)), 1) * inner)
    bi, bm = column(b_in[...], 0, hid), column(b_mid[...], 0, w_mid.shape[1])
    wi, wm = split(w_in[...].T), split(w_mid[...].T)
    width = w_out.shape[1]
    oh, ol = split(w_out[...])
    nt = ((1,), (1,))
    i = lax.broadcasted_iota(jnp.int32, (chans, width), 0)
    j = lax.broadcasted_iota(jnp.int32, (chans, width), 1)
    pick = jnp.where(j == i + first, 1.0, 0.0).astype(BF16)
    own = (mm(pick, oh, nt).astype(BF16), mm(pick, ol, nt).astype(BF16))
    dec = column(decay[...], first, chans)
    gain = jnp.sqrt(2.0 * dec / length)
    most = max(1, 2048 // inner)
    result = []
    for start, stop in parts:
        blocks = []
        for s0 in range(start, stop, most):
            some = range(s0, min(stop, s0 + most))
            cs, sn = [], []
            for s in some:
                a, b = sc[:, s : s + 1], ss[:, s : s + 1]
                cs.append(rc * a - rs * b)
                sn.append(rs * a + rc * b)
            feats = jnp.concatenate([jnp.concatenate(cs, 1), jnp.concatenate(sn, 1)], 0)
            h = jnp.maximum(dot3(wi, split(feats)) + bi, 0.0)
            h = jnp.maximum(dot3(wm, split(h)) + bm, 0.0)
            shape = dot3(own, split(h))
            n = (lax.broadcasted_iota(jnp.int32, shape.shape, 1) + s0 * inner).astype(F32) / length
            kern = shape * (jnp.exp(-dec * n) * gain)
            blocks += [kern[:, q * inner : (q + 1) * inner] for q in range(len(some))]
        result.append(blocks)
    return result


def body(
    n, m, groups,
    tok_hbm, gate_hbm, value_hbm, out_hbm, turn_hbm, mat_hbm,
    wave_hbm, w_in_hbm, b_in_hbm, w_mid_hbm, b_mid_hbm, w_out_hbm, decay_hbm,
    result,
    wave, w_in, b_in, w_mid, b_mid, w_out, decay,
    tok, gate_w, value_w, out_w, turn, mat,
    sent, got, got_x, own_out, own_in, cross_out, cross_in, spec_ref, prod_ref, part_out, part_in,
    load_sem, up_sem, all_sem, tok_send, tok_recv,
    a_send, a_recv, x_send, x_recv, b_send, b_recv, y_send, y_recv, p_send, p_recv,
):
    me, mine = lax.axis_index("seq"), lax.axis_index("chan")
    rows, depth = tok_hbm.shape
    width = value_w.shape[1]
    half = n // 2
    side, idx = me // half, lax.rem(me, half)
    chans = width // half

    def flipped(at, i, count):
        if count & (count - 1):
            return lax.rem(at + i, count)
        bit, to = 1, 0
        while bit < count:
            here = lax.rem(at // bit, 2)
            to = to + (1 - here if i & bit else here) * bit
            bit *= 2
        return to

    barrier = pltpu.get_barrier_semaphore()
    lead = m - 1
    for i in range(n - 1, 0, -1):
        pl.semaphore_signal(barrier, inc=1, device_id={"seq": flipped(me, i, n), "chan": lead}, device_id_type=MESH)

    @pl.when(mine == lead)
    def _():
        pl.semaphore_signal(barrier, inc=1, device_id={"chan": 1 - lead}, device_id_type=MESH)

    loads = [
        pltpu.make_async_copy(src, dst, load_sem.at[i])
        for i, (src, dst) in enumerate(
            [
                (tok_hbm, tok.at[mine]), (value_hbm, value_w), (gate_hbm, gate_w), (mat_hbm, mat), (turn_hbm, turn), (out_hbm, out_w),
                (wave_hbm, wave), (w_in_hbm, w_in), (b_in_hbm, b_in), (w_mid_hbm, w_mid), (b_mid_hbm, b_mid), (w_out_hbm, w_out), (decay_hbm, decay),
            ]
        )
    ]
    for c in loads:
        c.start()

    def remote(src, dst, send, recv, to):
        c = pltpu.make_async_remote_copy(
            src_ref=src, dst_ref=dst, send_sem=send, recv_sem=recv, device_id=to, device_id_type=MESH
        )
        c.start()
        return c

    def drain(block, sem):
        pltpu.make_async_copy(block, block, sem).wait()

    def peers(ref, g):
        return ref.at[pl.ds(0, half - 1), pl.ds(groups[g][0], groups[g][1]), :]

    def lines(ref, who, g):
        first, count = groups[g]
        return ref.at[pl.ds(pl.multiple_of(who * chans + first, 8), count), :]

    def project(who, w_ref):
        where = pl.ds(pl.multiple_of(who * depth, 8), depth)
        return dot3(split(tok[who]), split(w_ref[where, :]))

    @pl.when(mine != lead)
    def _():
        pl.semaphore_wait(barrier, 1)
        pl.semaphore_signal(up_sem, inc=1, device_id={"chan": lead}, device_id_type=MESH)

    @pl.when(mine == lead)
    def _():
        pl.semaphore_wait(up_sem, 1)

    loads[0].wait()
    tok_copies = []
    for i in range(1, m):
        there = {"chan": lax.rem(mine + i, m)}
        tok_copies.append(remote(tok.at[mine], tok.at[mine], tok_send.at[i], tok_recv.at[i], there))
    loads[1].wait()
    value_sum = project(mine, value_w)
    for i in range(1, m):
        tok_copies[i - 1].wait_recv()
        value_sum = value_sum + project(lax.rem(mine + m - i, m), value_w)
    sent[...] = silu(value_sum).T

    @pl.when(mine == lead)
    def _():
        pl.semaphore_wait(barrier, m * (n - 1))
        pl.semaphore_signal(all_sem, inc=1, device_id={"chan": 1 - lead}, device_id_type=MESH)

    @pl.when(mine != lead)
    def _():
        pl.semaphore_wait(all_sem, 1)

    lower, by_value = side == 0, mine == lead
    near = sorted(range(half), key=lambda i: (bin(i % max(1, half // 2)).count("1"), i))

    @pl.when(jnp.logical_and(lower, by_value))
    def _():
        for g, (first, count) in enumerate(groups):
            for i in near:
                to = flipped(idx, i, half)
                there = got_x.at[idx, pl.ds(first, count), :]
                remote(lines(sent, to, g), there, x_send, x_recv.at[g], {"seq": half + to})

    for g, (first, count) in enumerate(groups):
        for i in range(half - 1, 0, -1):
            to = flipped(idx, i, half)
            there = got.at[idx, pl.ds(first, count), :]
            remote(lines(sent, to, g), there, a_send, a_recv.at[g], {"seq": side * half + to})
        got[idx, first : first + count, :] = lines(sent, idx, g)[...]

    for c in loads[3:5] + loads[6:]:
        c.wait()
    low, high = position_blocks(
        n * rows, rows, [(0, half), (half, n)], idx * chans, chans, wave, w_in, b_in, w_mid, b_mid, w_out, decay
    )
    kern, k_cross = [], []
    for first, count in groups:
        own = forward([b[first : first + count] for b in low], turn, mat)
        far = forward([b[first : first + count] for b in high], turn, mat)
        kern.append(own)
        k_cross.append(jnp.concatenate([far[:, :rows] - own[:, rows:], far[:, rows:] + own[:, :rows]], axis=1))

    def part(ref, g):
        first, count = groups[g]
        return [ref[s, first : first + count, :] for s in range(half)]

    for g, (first, count) in enumerate(groups):
        drain(peers(got, g), a_recv.at[g])
        spec = forward(part(got, g), turn, mat)
        spec_ref[g] = spec
        prod_ref[g] = cmul(spec, kern[g])

        @pl.when(jnp.logical_and(lower, jnp.logical_not(by_value)))
        def _():
            for s, y in enumerate(backward(cmul(spec_ref[g], k_cross[g]), half, turn, mat)):
                cross_out[s, first : first + count, :] = y
            for i in near:
                to = flipped(idx, i, half)
                here, there = cross_out.at[to, pl.ds(first, count), :], cross_in.at[idx, pl.ds(first, count), :]
                remote(here, there, y_send, y_recv.at[g], {"seq": half + to})

        @pl.when(jnp.logical_and(side == 1, by_value))
        def _():
            drain(got_x.at[:, pl.ds(first, count), :], x_recv.at[g])
            prod_ref[g] = prod_ref[g] + cmul(forward(part(got_x, g), turn, mat), k_cross[g])

        for s, y in enumerate(backward(prod_ref[g], half, turn, mat)):
            own_out[s, first : first + count, :] = y
        for i in range(half - 1, 0, -1):
            to = flipped(idx, i, half)
            here, there = own_out.at[to, pl.ds(first, count), :], own_in.at[idx, pl.ds(first, count), :]
            remote(here, there, b_send, b_recv.at[g], {"seq": side * half + to})
        own_in[idx, first : first + count, :] = own_out[idx, first : first + count, :]

    loads[2].wait()
    gate_sum = project(mine, gate_w)
    for i in range(1, m):
        gate_sum = gate_sum + project(lax.rem(mine + m - i, m), gate_w)
    gate_lines = silu(gate_sum).T.reshape(half, chans, rows)
    loads[5].wait()
    other = lax.rem(mine + 1, m)
    step = part_out.shape[2]

    def partial(mixed, g, start, size):
        first, count = groups[g]
        cols = pl.ds(pl.multiple_of(start, 128), size)
        some = out_w[:, cols].reshape(half, chans, size)[:, first : first + count, :]
        return dot3(mixed, split(some.reshape(half * count, size)))

    sums = [0.0, 0.0]
    for g, (first, count) in enumerate(groups):
        drain(peers(own_in, g), b_recv.at[g])

        @pl.when(jnp.logical_and(side == 1, jnp.logical_not(by_value)))
        def _():
            drain(cross_in.at[:, pl.ds(first, count), :], y_recv.at[g])
            own_in[:, first : first + count, :] = (
                own_in[:, first : first + count, :] + cross_in[:, first : first + count, :]
            )

        some = slice(first, first + count)
        mixed = split((gate_lines[:, some, :] * own_in[:, some, :]).reshape(half * count, rows).T)
        if g < len(groups) - 1:
            sums = [t + partial(mixed, g, who * depth, depth) for t, who in zip(sums, (mine, other))]

    for q in range(depth // step):
        ahead = sums[1][:, q * step : (q + 1) * step] if len(groups) > 1 else 0.0
        part_out[q] = ahead + partial(mixed, len(groups) - 1, other * depth + q * step, step)
        remote(part_out.at[q], part_in.at[q], p_send, p_recv, {"chan": other})
    total = sums[0] + partial(mixed, len(groups) - 1, mine * depth, depth)
    drain(part_in, p_recv)
    for q in range(depth // step):
        result[:, q * step : (q + 1) * step] = total[:, q * step : (q + 1) * step] + part_in[q]
    for g in range(len(groups)):
        drain(peers(got, g), a_send)
        drain(peers(own_in, g), b_send)

    @pl.when(jnp.logical_and(lower, by_value))
    def _():
        drain(got_x, x_send)

    @pl.when(jnp.logical_and(lower, jnp.logical_not(by_value)))
    def _():
        drain(cross_out, y_send)

    for c in tok_copies:
        c.wait_send()
    drain(part_out, p_send)


def on_device(
    tokens, gate_weight, value_weight, output_weight, wave_numbers,
    position_in, bias_in, position_mid, bias_mid, position_out, decay_rate,
):
    n, m = lax.axis_size("seq"), lax.axis_size("chan")
    rows, depth = tokens.shape
    width = gate_weight.shape[1]
    half = n // 2
    chans = width // half
    count = chans // 2 if chans % 16 == 0 else chans
    groups = [(first, count) for first in range(0, chans, count)]
    assert m == 2 and n % 2 == 0
    turns, mats = tables(half, rows)
    hbm = pl.BlockSpec(memory_space=pl.ANY)
    vmem = pl.BlockSpec(memory_space=pltpu.VMEM)
    dma = pltpu.SemaphoreType.DMA
    return pl.pallas_call(
        functools.partial(body, n, m, groups),
        out_shape=pltpu.VMEM((rows, depth), F32),
        in_specs=[hbm] * 13,
        out_specs=vmem,
        scratch_shapes=[
            pltpu.VMEM((1, wave_numbers.shape[0]), jnp.int32),
            pltpu.VMEM(position_in.shape, F32),
            pltpu.VMEM((1, bias_in.shape[0]), F32),
            pltpu.VMEM(position_mid.shape, F32),
            pltpu.VMEM((1, bias_mid.shape[0]), F32),
            pltpu.VMEM(position_out.shape, F32),
            pltpu.VMEM((1, width), F32),
            pltpu.VMEM((m, rows, depth), F32),
            pltpu.VMEM(gate_weight.shape, F32),
            pltpu.VMEM(value_weight.shape, F32),
            pltpu.VMEM(output_weight.shape, F32),
            pltpu.VMEM(turns.shape, F32),
            pltpu.VMEM(mats.shape, BF16),
            pltpu.VMEM((width, rows), F32),
            pltpu.VMEM((half, chans, rows), F32),
            pltpu.VMEM((half, chans, rows), F32),
            pltpu.VMEM((half, chans, rows), F32),
            pltpu.VMEM((half, chans, rows), F32),
            pltpu.VMEM((half, chans, rows), F32),
            pltpu.VMEM((half, chans, rows), F32),
            pltpu.VMEM((len(groups), half * count, 2 * rows), F32),
            pltpu.VMEM((len(groups), half * count, 2 * rows), F32),
            pltpu.VMEM((depth // 128, rows, 128), F32),
            pltpu.VMEM((depth // 128, rows, 128), F32),
            dma((13,)),
            pltpu.SemaphoreType.REGULAR,
            pltpu.SemaphoreType.REGULAR,
            dma((m,)), dma((m,)),
            dma, dma((len(groups),)), dma, dma((len(groups),)),
            dma, dma((len(groups),)), dma, dma((len(groups),)),
            dma, dma,
        ],
        compiler_params=pltpu.CompilerParams(collective_id=0, has_side_effects=True),
    )(
        tokens, gate_weight, value_weight, output_weight, jnp.asarray(turns), jnp.asarray(mats),
        wave_numbers[None, :], position_in, bias_in[None, :], position_mid, bias_mid[None, :],
        position_out, decay_rate[None, :],
    )


def solution(mesh):
    placed = (
        P("seq", "chan"), P(None, "chan"), P(None, "chan"), P("chan", None),
        P(), P(), P(), P(), P(), P(None, "chan"), P("chan"),
    )
    return jax.shard_map(
        on_device, mesh=mesh, in_specs=placed, out_specs=P("seq", "chan"), check_vma=False
    )
```

time: 23.3 us -> 21.7 us (0.931)
  the two profiles are of different devices: /device:TPU:0 before, /device:TPU:17 now
where the time goes in v2:
time: 21.7 us; the launch traced here: 21.5 us
  Pallas kernels  20.8 us (96%)
  local copies, waits for them, and re-layouts  0.71 us (3%)
    pallas_call x1, Pallas kernels, on_device(): pl.pallas_call(functools.partial(body, n, m, groups), out_shape=pltpu.VME...  20.8 us
    unnamed x1, local copies, waits for them, and re-layouts  0.71 us

profile of v2, /device:TPU:17, one launch (start us, length us, event | category | flops | bytes accessed | tf_op | source)
XLA Modules:
  0.0 21.5 jit_solution(17191131073964378255)
XLA Ops:
  0.0 20.8 %shard_map.127 = f32[128,512]{1,0:T(8,128)S(1)} custom-call(f32[128,512]{1,0:T(8,128)} %tok_hbm.1, f32[1024,512]{1,0:T(8,128)} %gate_hbm.1, f32[1024,512]{1,0:T(8,128)} %value_hbm.1, f32[512,1024]{1,0:T(8,128)} %out_hbm.1, f32[16,128]{1,0:T(8,128)} %constant.4.clone.turn_hbm, bf16[4,256,256]{2,1,0:T(8,128)(2,1)} %constant.5.clone.mat_hbm, s32[1,32]{1,0:T(1,128)} %bitcast.5, ...), custom_call_target="tpu_custom_call" | custom-call | tf_op jit(solution)/shard_map/pallas_call | solution.py:397
  20.8 0.7 %copy.15 = f32[128,512]{1,0:T(8,128)} copy(f32[128,512]{1,0:T(8,128)S(1)} %shard_map.127) | data formatting | bytes 524288

commit v3 on v2

--- a/solution.py
+++ b/solution.py
@@ -167,8 +167,8 @@
     result,
     wave, w_in, b_in, w_mid, b_mid, w_out, decay,
     tok, gate_w, value_w, out_w, turn, mat,
-    sent, got, got_x, own_out, own_in, cross_out, cross_in, spec_ref, prod_ref, part_out, part_in,
-    load_sem, up_sem, all_sem, tok_send, tok_recv,
+    sent, got, got_x, own_out, own_in, cross_out, cross_in, spec_ref, prod_ref, w_high, w_low, part_out, part_in,
+    load_sem, up_sem, all_sem, far_sem, tok_send, tok_recv,
     a_send, a_recv, x_send, x_recv, b_send, b_recv, y_send, y_recv, p_send, p_recv,
 ):
     me, mine = lax.axis_index("seq"), lax.axis_index("chan")
@@ -189,9 +189,18 @@
         return to
 
     barrier = pltpu.get_barrier_semaphore()
-    lead = m - 1
-    for i in range(n - 1, 0, -1):
-        pl.semaphore_signal(barrier, inc=1, device_id={"seq": flipped(me, i, n), "chan": lead}, device_id_type=MESH)
+    lead, quarter = m - 1, half // 2
+    lower, by_value = side == 0, mine == lead
+    first_z, second_z = jnp.logical_and(lower, idx < quarter), jnp.logical_and(lower, idx >= quarter)
+    by_result = jnp.logical_not(by_value)
+    for i in range(half - 1, 0, -1):
+        to = side * half + flipped(idx, i, half)
+        pl.semaphore_signal(barrier, inc=1, device_id={"seq": to, "chan": lead}, device_id_type=MESH)
+
+    @pl.when(jnp.logical_not(lower))
+    def _():
+        for to in range(quarter, half):
+            pl.semaphore_signal(barrier, inc=1, device_id={"seq": to, "chan": lead}, device_id_type=MESH)
 
     @pl.when(mine == lead)
     def _():
@@ -226,9 +235,11 @@
         first, count = groups[g]
         return ref.at[pl.ds(pl.multiple_of(who * chans + first, 8), count), :]
 
+    def weight(who, w_ref):
+        return split(w_ref[pl.ds(pl.multiple_of(who * depth, 8), depth), :])
+
     def project(who, w_ref):
-        where = pl.ds(pl.multiple_of(who * depth, 8), depth)
-        return dot3(split(tok[who]), split(w_ref[where, :]))
+        return dot3(split(tok[who]), weight(who, w_ref))
 
     @pl.when(mine != lead)
     def _():
@@ -246,30 +257,46 @@
         tok_copies.append(remote(tok.at[mine], tok.at[mine], tok_send.at[i], tok_recv.at[i], there))
     loads[1].wait()
     value_sum = project(mine, value_w)
-    for i in range(1, m):
-        tok_copies[i - 1].wait_recv()
-        value_sum = value_sum + project(lax.rem(mine + m - i, m), value_w)
+    ahead = weight(1 - mine, value_w)
+    tok_copies[0].wait_recv()
+    value_sum = value_sum + dot3(split(tok[1 - mine]), ahead)
     sent[...] = silu(value_sum).T
 
-    @pl.when(mine == lead)
-    def _():
-        pl.semaphore_wait(barrier, m * (n - 1))
-        pl.semaphore_signal(all_sem, inc=1, device_id={"chan": 1 - lead}, device_id_type=MESH)
-
-    @pl.when(mine != lead)
-    def _():
-        pl.semaphore_wait(all_sem, 1)
-
-    lower, by_value = side == 0, mine == lead
     near = sorted(range(half), key=lambda i: (bin(i % max(1, half // 2)).count("1"), i))
 
-    @pl.when(jnp.logical_and(lower, by_value))
-    def _():
+    def tell(sem, **who):
+        pl.semaphore_signal(sem, inc=1, device_id=who, device_id_type=MESH)
+
+    def cross_values():
         for g, (first, count) in enumerate(groups):
             for i in near:
                 to = flipped(idx, i, half)
                 there = got_x.at[idx, pl.ds(first, count), :]
                 remote(lines(sent, to, g), there, x_send, x_recv.at[g], {"seq": half + to})
+
+    @pl.when(jnp.logical_and(by_value, jnp.logical_not(second_z)))
+    def _():
+        pl.semaphore_wait(barrier, m * (half - 1))
+        tell(all_sem, chan=1 - lead)
+
+        @pl.when(jnp.logical_and(lower, idx + quarter < half))
+        def _():
+            tell(all_sem, seq=idx + quarter, chan=1 - lead)
+
+    @pl.when(jnp.logical_and(by_value, second_z))
+    def _():
+        pl.semaphore_wait(barrier, m * (n - 1))
+        tell(far_sem, chan=1 - lead)
+
+        @pl.when(idx >= quarter)
+        def _():
+            tell(far_sem, seq=idx - quarter)
+
+        cross_values()
+
+    @pl.when(by_result)
+    def _():
+        pl.semaphore_wait(all_sem, 1)
 
     for g, (first, count) in enumerate(groups):
         for i in range(half - 1, 0, -1):
@@ -277,6 +304,12 @@
             there = got.at[idx, pl.ds(first, count), :]
             remote(lines(sent, to, g), there, a_send, a_recv.at[g], {"seq": side * half + to})
         got[idx, first : first + count, :] = lines(sent, idx, g)[...]
+
+    @pl.when(jnp.logical_and(by_value, first_z))
+    def _():
+        pl.semaphore_wait(far_sem, 1)
+        tell(far_sem, chan=1 - lead)
+        cross_values()
 
     for c in loads[3:5] + loads[6:]:
         c.wait()
@@ -300,15 +333,6 @@
         spec_ref[g] = spec
         prod_ref[g] = cmul(spec, kern[g])
 
-        @pl.when(jnp.logical_and(lower, jnp.logical_not(by_value)))
-        def _():
-            for s, y in enumerate(backward(cmul(spec_ref[g], k_cross[g]), half, turn, mat)):
-                cross_out[s, first : first + count, :] = y
-            for i in near:
-                to = flipped(idx, i, half)
-                here, there = cross_out.at[to, pl.ds(first, count), :], cross_in.at[idx, pl.ds(first, count), :]
-                remote(here, there, y_send, y_recv.at[g], {"seq": half + to})
-
         @pl.when(jnp.logical_and(side == 1, by_value))
         def _():
             drain(got_x.at[:, pl.ds(first, count), :], x_recv.at[g])
@@ -322,26 +346,37 @@
             remote(here, there, b_send, b_recv.at[g], {"seq": side * half + to})
         own_in[idx, first : first + count, :] = own_out[idx, first : first + count, :]
 
+        @pl.when(jnp.logical_and(lower, by_result))
+        def _():
+            for s, y in enumerate(backward(cmul(spec_ref[g], k_cross[g]), half, turn, mat)):
+                cross_out[s, first : first + count, :] = y
+            if g == 0:
+                pl.semaphore_wait(far_sem, 1)
+            for i in near:
+                to = flipped(idx, i, half)
+                here, there = cross_out.at[to, pl.ds(first, count), :], cross_in.at[idx, pl.ds(first, count), :]
+                remote(here, there, y_send, y_recv.at[g], {"seq": half + to})
+
     loads[2].wait()
     gate_sum = project(mine, gate_w)
     for i in range(1, m):
         gate_sum = gate_sum + project(lax.rem(mine + m - i, m), gate_w)
     gate_lines = silu(gate_sum).T.reshape(half, chans, rows)
     loads[5].wait()
+    for g, (first, count) in enumerate(groups):
+        some = out_w[...].reshape(half, chans, m * depth)[:, first : first + count, :]
+        w_high[g], w_low[g] = split(some.reshape(half * count, m * depth))
     other = lax.rem(mine + 1, m)
-    step = part_out.shape[2]
 
     def partial(mixed, g, start, size):
-        first, count = groups[g]
         cols = pl.ds(pl.multiple_of(start, 128), size)
-        some = out_w[:, cols].reshape(half, chans, size)[:, first : first + count, :]
-        return dot3(mixed, split(some.reshape(half * count, size)))
+        return dot3(mixed, (w_high[g, :, cols], w_low[g, :, cols]))
 
     sums = [0.0, 0.0]
     for g, (first, count) in enumerate(groups):
         drain(peers(own_in, g), b_recv.at[g])
 
-        @pl.when(jnp.logical_and(side == 1, jnp.logical_not(by_value)))
+        @pl.when(jnp.logical_and(side == 1, by_result))
         def _():
             drain(cross_in.at[:, pl.ds(first, count), :], y_recv.at[g])
             own_in[:, first : first + count, :] = (
@@ -353,14 +388,11 @@
         if g < len(groups) - 1:
             sums = [t + partial(mixed, g, who * depth, depth) for t, who in zip(sums, (mine, other))]
 
-    for q in range(depth // step):
-        ahead = sums[1][:, q * step : (q + 1) * step] if len(groups) > 1 else 0.0
-        part_out[q] = ahead + partial(mixed, len(groups) - 1, other * depth + q * step, step)
-        remote(part_out.at[q], part_in.at[q], p_send, p_recv, {"chan": other})
+    part_out[...] = sums[1] + partial(mixed, len(groups) - 1, other * depth, depth)
+    remote(part_out, part_in, p_send, p_recv, {"chan": other})
     total = sums[0] + partial(mixed, len(groups) - 1, mine * depth, depth)
     drain(part_in, p_recv)
-    for q in range(depth // step):
-        result[:, q * step : (q + 1) * step] = total[:, q * step : (q + 1) * step] + part_in[q]
+    result[...] = total + part_in[...]
     for g in range(len(groups)):
         drain(peers(got, g), a_send)
         drain(peers(own_in, g), b_send)
@@ -369,7 +401,7 @@
     def _():
         drain(got_x, x_send)
 
-    @pl.when(jnp.logical_and(lower, jnp.logical_not(by_value)))
+    @pl.when(jnp.logical_and(lower, by_result))
     def _():
         drain(cross_out, y_send)
 
@@ -422,9 +454,12 @@
             pltpu.VMEM((half, chans, rows), F32),
             pltpu.VMEM((len(groups), half * count, 2 * rows), F32),
             pltpu.VMEM((len(groups), half * count, 2 * rows), F32),
-            pltpu.VMEM((depth // 128, rows, 128), F32),
-            pltpu.VMEM((depth // 128, rows, 128), F32),
+            pltpu.VMEM((len(groups), half * count, m * depth), BF16),
+            pltpu.VMEM((len(groups), half * count, m * depth), BF16),
+            pltpu.VMEM((rows, depth), F32),
+            pltpu.VMEM((rows, depth), F32),
             dma((13,)),
+            pltpu.SemaphoreType.REGULAR,
             pltpu.SemaphoreType.REGULAR,
             pltpu.SemaphoreType.REGULAR,
             dma((m,)), dma((m,)),

time: 21.7 us -> 20.5 us (0.945)
  Pallas kernels: 20.8 us -> 19.6 us
    pallas_call x1, Pallas kernels: 20.8 us -> 19.6 us  [on_device(): pl.pallas_call(functools.partial(body, n, m, groups), out_shape=pltpu.VME...]
where the time goes in v3:
time: 20.5 us; the launch traced here: 20.3 us
  Pallas kernels  19.6 us (96%)
  local copies, waits for them, and re-layouts  0.71 us (3%)
    pallas_call x1, Pallas kernels, on_device(): pl.pallas_call(functools.partial(body, n, m, groups), out_shape=pltpu.VME...  19.6 us
    unnamed x1, local copies, waits for them, and re-layouts  0.71 us

profile of v3, /device:TPU:17, one launch (start us, length us, event | category | flops | bytes accessed | tf_op | source)
XLA Modules:
  0.0 20.3 jit_solution(1389003397686887352)
XLA Ops:
  0.0 19.6 %shard_map.127 = f32[128,512]{1,0:T(8,128)S(1)} custom-call(f32[128,512]{1,0:T(8,128)} %tok_hbm.1, f32[1024,512]{1,0:T(8,128)} %gate_hbm.1, f32[1024,512]{1,0:T(8,128)} %value_hbm.1, f32[512,1024]{1,0:T(8,128)} %out_hbm.1, f32[16,128]{1,0:T(8,128)} %constant.4.clone.turn_hbm, bf16[4,256,256]{2,1,0:T(8,128)(2,1)} %constant.5.clone.mat_hbm, s32[1,32]{1,0:T(1,128)} %bitcast.5, ...), custom_call_target="tpu_custom_call" | custom-call | tf_op jit(solution)/shard_map/pallas_call | solution.py:429
  19.6 0.7 %copy.15 = f32[128,512]{1,0:T(8,128)} copy(f32[128,512]{1,0:T(8,128)S(1)} %shard_map.127) | data formatting | bytes 524288

commit v4 on v3

--- a/solution.py
+++ b/solution.py
@@ -168,9 +168,9 @@
     wave, w_in, b_in, w_mid, b_mid, w_out, decay,
     tok, gate_w, value_w, out_w, turn, mat,
     sent, got, got_x, own_out, own_in, cross_out, cross_in, spec_ref, prod_ref, w_high, w_low, part_out, part_in,
-    load_sem, up_sem, all_sem, far_sem, tok_send, tok_recv,
-    a_send, a_recv, x_send, x_recv, b_send, b_recv, y_send, y_recv, p_send, p_recv,
+    up_sem, all_sem, far_sem, tok_recv, a_recv, x_recv, b_recv, y_recv, p_recv, load_sem, send_sems,
 ):
+    tok_send, a_send, x_send, b_send, y_send, p_send = (send_sems.at[i] for i in range(6))
     me, mine = lax.axis_index("seq"), lax.axis_index("chan")
     rows, depth = tok_hbm.shape
     width = value_w.shape[1]
@@ -188,24 +188,6 @@
             bit *= 2
         return to
 
-    barrier = pltpu.get_barrier_semaphore()
-    lead, quarter = m - 1, half // 2
-    lower, by_value = side == 0, mine == lead
-    first_z, second_z = jnp.logical_and(lower, idx < quarter), jnp.logical_and(lower, idx >= quarter)
-    by_result = jnp.logical_not(by_value)
-    for i in range(half - 1, 0, -1):
-        to = side * half + flipped(idx, i, half)
-        pl.semaphore_signal(barrier, inc=1, device_id={"seq": to, "chan": lead}, device_id_type=MESH)
-
-    @pl.when(jnp.logical_not(lower))
-    def _():
-        for to in range(quarter, half):
-            pl.semaphore_signal(barrier, inc=1, device_id={"seq": to, "chan": lead}, device_id_type=MESH)
-
-    @pl.when(mine == lead)
-    def _():
-        pl.semaphore_signal(barrier, inc=1, device_id={"chan": 1 - lead}, device_id_type=MESH)
-
     loads = [
         pltpu.make_async_copy(src, dst, load_sem.at[i])
         for i, (src, dst) in enumerate(
@@ -215,7 +197,28 @@
             ]
         )
     ]
-    for c in loads:
+    for c in loads[:2]:
+        c.start()
+
+    barrier = pltpu.get_barrier_semaphore()
+    lead, quarter = m - 1, half // 2
+    lower, by_value = side == 0, mine == lead
+    first_z, second_z = jnp.logical_and(lower, idx < quarter), jnp.logical_and(lower, idx >= quarter)
+    by_result = jnp.logical_not(by_value)
+    @pl.when(mine == lead)
+    def _():
+        pl.semaphore_signal(barrier, inc=1, device_id={"chan": 1 - lead}, device_id_type=MESH)
+
+    for i in range(half - 1, 0, -1):
+        to = side * half + flipped(idx, i, half)
+        pl.semaphore_signal(barrier, inc=1, device_id={"seq": to, "chan": lead}, device_id_type=MESH)
+
+    @pl.when(jnp.logical_not(lower))
+    def _():
+        for to in range(quarter, half):
+            pl.semaphore_signal(barrier, inc=1, device_id={"seq": to, "chan": lead}, device_id_type=MESH)
+
+    for c in loads[2:]:
         c.start()
 
     def remote(src, dst, send, recv, to):
@@ -251,15 +254,17 @@
         pl.semaphore_wait(up_sem, 1)
 
     loads[0].wait()
-    tok_copies = []
-    for i in range(1, m):
-        there = {"chan": lax.rem(mine + i, m)}
-        tok_copies.append(remote(tok.at[mine], tok.at[mine], tok_send.at[i], tok_recv.at[i], there))
+    pieces = [pl.ds(first, depth // 2) for first in (0, depth // 2)]
+    for i, piece in enumerate(pieces):
+        part_of = tok.at[mine, :, piece]
+        remote(part_of, part_of, tok_send, tok_recv.at[i], {"chan": 1 - mine})
     loads[1].wait()
     value_sum = project(mine, value_w)
     ahead = weight(1 - mine, value_w)
-    tok_copies[0].wait_recv()
-    value_sum = value_sum + dot3(split(tok[1 - mine]), ahead)
+    for i, piece in enumerate(pieces):
+        drain(tok.at[mine, :, piece], tok_recv.at[i])
+        there = slice(i * (depth // 2), (i + 1) * (depth // 2))
+        value_sum = value_sum + dot3(split(tok[1 - mine, :, there]), tuple(w[there] for w in ahead))
     sent[...] = silu(value_sum).T
 
     near = sorted(range(half), key=lambda i: (bin(i % max(1, half // 2)).count("1"), i))
@@ -352,7 +357,7 @@
                 cross_out[s, first : first + count, :] = y
             if g == 0:
                 pl.semaphore_wait(far_sem, 1)
-            for i in near:
+            for i in reversed(near):
                 to = flipped(idx, i, half)
                 here, there = cross_out.at[to, pl.ds(first, count), :], cross_in.at[idx, pl.ds(first, count), :]
                 remote(here, there, y_send, y_recv.at[g], {"seq": half + to})
@@ -405,9 +410,14 @@
     def _():
         drain(cross_out, y_send)
 
-    for c in tok_copies:
-        c.wait_send()
+    drain(tok.at[mine], tok_send)
     drain(part_out, p_send)
+
+
+def scoped_body(*args):
+    pl.run_scoped(
+        functools.partial(body, *args), pltpu.SemaphoreType.DMA((13,)), pltpu.SemaphoreType.DMA((6,))
+    )
 
 
 def on_device(
@@ -427,7 +437,7 @@
     vmem = pl.BlockSpec(memory_space=pltpu.VMEM)
     dma = pltpu.SemaphoreType.DMA
     return pl.pallas_call(
-        functools.partial(body, n, m, groups),
+        functools.partial(scoped_body, n, m, groups),
         out_shape=pltpu.VMEM((rows, depth), F32),
         in_specs=[hbm] * 13,
         out_specs=vmem,
@@ -458,14 +468,12 @@
             pltpu.VMEM((len(groups), half * count, m * depth), BF16),
             pltpu.VMEM((rows, depth), F32),
             pltpu.VMEM((rows, depth), F32),
-            dma((13,)),
             pltpu.SemaphoreType.REGULAR,
             pltpu.SemaphoreType.REGULAR,
             pltpu.SemaphoreType.REGULAR,
-            dma((m,)), dma((m,)),
-            dma, dma((len(groups),)), dma, dma((len(groups),)),
-            dma, dma((len(groups),)), dma, dma((len(groups),)),
-            dma, dma,
+            dma((2,)),
+            dma((len(groups),)), dma((len(groups),)), dma((len(groups),)), dma((len(groups),)),
+            dma,
         ],
         compiler_params=pltpu.CompilerParams(collective_id=0, has_side_effects=True),
     )(

time: 20.5 us -> 20.1 us (0.980)
  Pallas kernels: 19.6 us -> 19.1 us
    pallas_call x1, Pallas kernels: 19.6 us -> 19.1 us  [on_device(): pl.pallas_call(functools.partial(scoped_body, n, m, groups), out_shape=pl...]
where the time goes in v4:
time: 20.1 us; the launch traced here: 19.8 us
  Pallas kernels  19.1 us (95%)
  local copies, waits for them, and re-layouts  0.71 us (4%)
    pallas_call x1, Pallas kernels, on_device(): pl.pallas_call(functools.partial(scoped_body, n, m, groups), out_shape=pl...  19.1 us
    unnamed x1, local copies, waits for them, and re-layouts  0.71 us

profile of v4, /device:TPU:17, one launch (start us, length us, event | category | flops | bytes accessed | tf_op | source)
XLA Modules:
  0.0 19.8 jit_solution(3036895851431969689)
XLA Ops:
  0.0 19.1 %shard_map.127 = f32[128,512]{1,0:T(8,128)S(1)} custom-call(f32[128,512]{1,0:T(8,128)} %args_0_.4, f32[1024,512]{1,0:T(8,128)} %args_1_.4, f32[1024,512]{1,0:T(8,128)} %args_2_.4, f32[512,1024]{1,0:T(8,128)} %args_3_.4, f32[16,128]{1,0:T(8,128)} %constant.4.clone.args_4_, bf16[4,256,256]{2,1,0:T(8,128)(2,1)} %constant.5.clone.args_5_, s32[1,32]{1,0:T(1,128)} %bitcast.5, ...), custom_call_target="tpu_custom_call" | custom-call | tf_op jit(solution)/shard_map/pallas_call | solution.py:439
  19.1 0.7 %copy.15 = f32[128,512]{1,0:T(8,128)} copy(f32[128,512]{1,0:T(8,128)S(1)} %shard_map.127) | data formatting | bytes 524288

commit v5 on v4

--- a/solution.py
+++ b/solution.py
@@ -168,7 +168,7 @@
     wave, w_in, b_in, w_mid, b_mid, w_out, decay,
     tok, gate_w, value_w, out_w, turn, mat,
     sent, got, got_x, own_out, own_in, cross_out, cross_in, spec_ref, prod_ref, w_high, w_low, part_out, part_in,
-    up_sem, all_sem, far_sem, tok_recv, a_recv, x_recv, b_recv, y_recv, p_recv, load_sem, send_sems,
+    up_sem, all_sem, near_sem, far_sem, tok_recv, a_recv, x_recv, b_recv, y_recv, p_recv, load_sem, send_sems,
 ):
     tok_send, a_send, x_send, b_send, y_send, p_send = (send_sems.at[i] for i in range(6))
     me, mine = lax.axis_index("seq"), lax.axis_index("chan")
@@ -204,6 +204,7 @@
     lead, quarter = m - 1, half // 2
     lower, by_value = side == 0, mine == lead
     first_z, second_z = jnp.logical_and(lower, idx < quarter), jnp.logical_and(lower, idx >= quarter)
+    third_z = jnp.logical_and(side == 1, idx < quarter)
     by_result = jnp.logical_not(by_value)
     @pl.when(mine == lead)
     def _():
@@ -213,10 +214,15 @@
         to = side * half + flipped(idx, i, half)
         pl.semaphore_signal(barrier, inc=1, device_id={"seq": to, "chan": lead}, device_id_type=MESH)
 
-    @pl.when(jnp.logical_not(lower))
+    @pl.when(third_z)
     def _():
         for to in range(quarter, half):
             pl.semaphore_signal(barrier, inc=1, device_id={"seq": to, "chan": lead}, device_id_type=MESH)
+
+    @pl.when(second_z)
+    def _():
+        to = me + quarter
+        pl.semaphore_signal(barrier, inc=1, device_id={"seq": to, "chan": lead}, device_id_type=MESH)
 
     for c in loads[2:]:
         c.start()
@@ -272,32 +278,37 @@
     def tell(sem, **who):
         pl.semaphore_signal(sem, inc=1, device_id=who, device_id_type=MESH)
 
-    def cross_values():
+    def cross_values(some):
         for g, (first, count) in enumerate(groups):
-            for i in near:
-                to = flipped(idx, i, half)
+            for i in sorted(range(quarter), key=lambda i: bin(i).count("1")):
+                to = some + flipped(lax.rem(idx, quarter), i, quarter)
                 there = got_x.at[idx, pl.ds(first, count), :]
                 remote(lines(sent, to, g), there, x_send, x_recv.at[g], {"seq": half + to})
 
-    @pl.when(jnp.logical_and(by_value, jnp.logical_not(second_z)))
+    @pl.when(jnp.logical_and(by_value, jnp.logical_not(jnp.logical_or(second_z, third_z))))
     def _():
         pl.semaphore_wait(barrier, m * (half - 1))
         tell(all_sem, chan=1 - lead)
 
-        @pl.when(jnp.logical_and(lower, idx + quarter < half))
+        @pl.when(lower)
         def _():
-            tell(all_sem, seq=idx + quarter, chan=1 - lead)
+            tell(all_sem, seq=me + quarter, chan=1 - lead)
+
+    @pl.when(jnp.logical_and(by_value, third_z))
+    def _():
+        pl.semaphore_wait(barrier, m * half)
+        tell(all_sem, chan=1 - lead)
+        tell(far_sem, seq=me - quarter)
 
     @pl.when(jnp.logical_and(by_value, second_z))
     def _():
-        pl.semaphore_wait(barrier, m * (n - 1))
+        pl.semaphore_wait(barrier, m * (half - 1 + quarter))
+        tell(near_sem, seq=me - quarter)
+        cross_values(0)
+        pl.semaphore_wait(far_sem, 1)
         tell(far_sem, chan=1 - lead)
-
-        @pl.when(idx >= quarter)
-        def _():
-            tell(far_sem, seq=idx - quarter)
-
-        cross_values()
+        tell(far_sem, seq=me - quarter)
+        cross_values(quarter)
 
     @pl.when(by_result)
     def _():
@@ -312,9 +323,11 @@
 
     @pl.when(jnp.logical_and(by_value, first_z))
     def _():
+        pl.semaphore_wait(near_sem, 1)
+        cross_values(0)
         pl.semaphore_wait(far_sem, 1)
         tell(far_sem, chan=1 - lead)
-        cross_values()
+        cross_values(quarter)
 
     for c in loads[3:5] + loads[6:]:
         c.wait()
@@ -431,7 +444,7 @@
     chans = width // half
     count = chans // 2 if chans % 16 == 0 else chans
     groups = [(first, count) for first in range(0, chans, count)]
-    assert m == 2 and n % 2 == 0
+    assert m == 2 and n % 4 == 0
     turns, mats = tables(half, rows)
     hbm = pl.BlockSpec(memory_space=pl.ANY)
     vmem = pl.BlockSpec(memory_space=pltpu.VMEM)
@@ -471,6 +484,7 @@
             pltpu.SemaphoreType.REGULAR,
             pltpu.SemaphoreType.REGULAR,
             pltpu.SemaphoreType.REGULAR,
+            pltpu.SemaphoreType.REGULAR,
             dma((2,)),
             dma((len(groups),)), dma((len(groups),)), dma((len(groups),)), dma((len(groups),)),
             dma,

time: 20.1 us -> 19.7 us (0.980)
  Pallas kernels: 19.1 us -> 18.6 us
    pallas_call x1, Pallas kernels: 19.1 us -> 18.6 us  [on_device(): pl.pallas_call(functools.partial(scoped_body, n, m, groups), out_shape=pl...]
where the time goes in v5:
time: 19.7 us; the launch traced here: 19.3 us
  Pallas kernels  18.6 us (94%)
  local copies, waits for them, and re-layouts  0.71 us (4%)
    pallas_call x1, Pallas kernels, on_device(): pl.pallas_call(functools.partial(scoped_body, n, m, groups), out_shape=pl...  18.6 us
    unnamed x1, local copies, waits for them, and re-layouts  0.71 us

profile of v5, /device:TPU:17, one launch (start us, length us, event | category | flops | bytes accessed | tf_op | source)
XLA Modules:
  0.0 19.3 jit_solution(2423951676232900440)
XLA Ops:
  0.0 18.6 %shard_map.127 = f32[128,512]{1,0:T(8,128)S(1)} custom-call(f32[128,512]{1,0:T(8,128)} %args_0_.4, f32[1024,512]{1,0:T(8,128)} %args_1_.4, f32[1024,512]{1,0:T(8,128)} %args_2_.4, f32[512,1024]{1,0:T(8,128)} %args_3_.4, f32[16,128]{1,0:T(8,128)} %constant.4.clone.args_4_, bf16[4,256,256]{2,1,0:T(8,128)(2,1)} %constant.5.clone.args_5_, s32[1,32]{1,0:T(1,128)} %bitcast.5, ...), custom_call_target="tpu_custom_call" | custom-call | tf_op jit(solution)/shard_map/pallas_call | solution.py:452
  18.6 0.7 %copy.15 = f32[128,512]{1,0:T(8,128)} copy(f32[128,512]{1,0:T(8,128)S(1)} %shard_map.127) | data formatting | bytes 524288

commit v6 on v5

--- a/solution.py
+++ b/solution.py
@@ -188,16 +188,18 @@
             bit *= 2
         return to
 
+    pieces = [pl.ds(first, depth // 2) for first in (0, depth // 2)]
     loads = [
         pltpu.make_async_copy(src, dst, load_sem.at[i])
         for i, (src, dst) in enumerate(
             [
-                (tok_hbm, tok.at[mine]), (value_hbm, value_w), (gate_hbm, gate_w), (mat_hbm, mat), (turn_hbm, turn), (out_hbm, out_w),
+                (tok_hbm.at[:, pieces[0]], tok.at[mine, :, pieces[0]]), (value_hbm, value_w), (gate_hbm, gate_w), (mat_hbm, mat), (turn_hbm, turn), (out_hbm, out_w),
                 (wave_hbm, wave), (w_in_hbm, w_in), (b_in_hbm, b_in), (w_mid_hbm, w_mid), (b_mid_hbm, b_mid), (w_out_hbm, w_out), (decay_hbm, decay),
+                (tok_hbm.at[:, pieces[1]], tok.at[mine, :, pieces[1]]),
             ]
         )
     ]
-    for c in loads[:2]:
+    for c in (loads[0], loads[13], loads[1]):
         c.start()
 
     barrier = pltpu.get_barrier_semaphore()
@@ -224,7 +226,7 @@
         to = me + quarter
         pl.semaphore_signal(barrier, inc=1, device_id={"seq": to, "chan": lead}, device_id_type=MESH)
 
-    for c in loads[2:]:
+    for c in loads[2:13]:
         c.start()
 
     def remote(src, dst, send, recv, to):
@@ -259,9 +261,8 @@
     def _():
         pl.semaphore_wait(up_sem, 1)
 
-    loads[0].wait()
-    pieces = [pl.ds(first, depth // 2) for first in (0, depth // 2)]
     for i, piece in enumerate(pieces):
+        loads[13 * i].wait()
         part_of = tok.at[mine, :, piece]
         remote(part_of, part_of, tok_send, tok_recv.at[i], {"chan": 1 - mine})
     loads[1].wait()
@@ -329,7 +330,7 @@
         tell(far_sem, chan=1 - lead)
         cross_values(quarter)
 
-    for c in loads[3:5] + loads[6:]:
+    for c in loads[3:5] + loads[6:13]:
         c.wait()
     low, high = position_blocks(
         n * rows, rows, [(0, half), (half, n)], idx * chans, chans, wave, w_in, b_in, w_mid, b_mid, w_out, decay
@@ -429,7 +430,7 @@
 
 def scoped_body(*args):
     pl.run_scoped(
-        functools.partial(body, *args), pltpu.SemaphoreType.DMA((13,)), pltpu.SemaphoreType.DMA((6,))
+        functools.partial(body, *args), pltpu.SemaphoreType.DMA((14,)), pltpu.SemaphoreType.DMA((6,))
     )
 
 

time: 19.7 us -> 19.6 us (level)
  no operation moved by 1% of the time
where the time goes in v6:
time: 19.6 us; the launch traced here: 19.3 us
  Pallas kernels  18.6 us (95%)
  local copies, waits for them, and re-layouts  0.71 us (4%)
    pallas_call x1, Pallas kernels, on_device(): pl.pallas_call(functools.partial(scoped_body, n, m, groups), out_shape=pl...  18.6 us
    unnamed x1, local copies, waits for them, and re-layouts  0.71 us

profile of v6, /device:TPU:17, one launch (start us, length us, event | category | flops | bytes accessed | tf_op | source)
XLA Modules:
  0.0 19.3 jit_solution(8395177053134455512)
XLA Ops:
  0.0 18.6 %shard_map.127 = f32[128,512]{1,0:T(8,128)S(1)} custom-call(f32[128,512]{1,0:T(8,128)} %args_0_.4, f32[1024,512]{1,0:T(8,128)} %args_1_.4, f32[1024,512]{1,0:T(8,128)} %args_2_.4, f32[512,1024]{1,0:T(8,128)} %args_3_.4, f32[16,128]{1,0:T(8,128)} %constant.4.clone.args_4_, bf16[4,256,256]{2,1,0:T(8,128)(2,1)} %constant.5.clone.args_5_, s32[1,32]{1,0:T(1,128)} %bitcast.5, ...), custom_call_target="tpu_custom_call" | custom-call | tf_op jit(solution)/shard_map/pallas_call | solution.py:453
  18.6 0.7 %copy.15 = f32[128,512]{1,0:T(8,128)} copy(f32[128,512]{1,0:T(8,128)S(1)} %shard_map.127) | data formatting | bytes 524288

commit v7 on v6

--- a/solution.py
+++ b/solution.py
@@ -281,7 +281,7 @@
 
     def cross_values(some):
         for g, (first, count) in enumerate(groups):
-            for i in sorted(range(quarter), key=lambda i: bin(i).count("1")):
+            for i in sorted(range(quarter), key=lambda i: -bin(i).count("1")):
                 to = some + flipped(lax.rem(idx, quarter), i, quarter)
                 there = got_x.at[idx, pl.ds(first, count), :]
                 remote(lines(sent, to, g), there, x_send, x_recv.at[g], {"seq": half + to})
@@ -306,10 +306,6 @@
         pl.semaphore_wait(barrier, m * (half - 1 + quarter))
         tell(near_sem, seq=me - quarter)
         cross_values(0)
-        pl.semaphore_wait(far_sem, 1)
-        tell(far_sem, chan=1 - lead)
-        tell(far_sem, seq=me - quarter)
-        cross_values(quarter)
 
     @pl.when(by_result)
     def _():
@@ -321,6 +317,13 @@
             there = got.at[idx, pl.ds(first, count), :]
             remote(lines(sent, to, g), there, a_send, a_recv.at[g], {"seq": side * half + to})
         got[idx, first : first + count, :] = lines(sent, idx, g)[...]
+
+    @pl.when(jnp.logical_and(by_value, second_z))
+    def _():
+        pl.semaphore_wait(far_sem, 1)
+        tell(far_sem, chan=1 - lead)
+        tell(far_sem, seq=me - quarter)
+        cross_values(quarter)
 
     @pl.when(jnp.logical_and(by_value, first_z))
     def _():

time: 19.6 us -> 19.3 us (0.985)
  no operation moved by 1% of the time
where the time goes in v7:
time: 19.3 us; the launch traced here: 19.2 us
  Pallas kernels  18.5 us (96%)
  local copies, waits for them, and re-layouts  0.71 us (4%)
    pallas_call x1, Pallas kernels, on_device(): pl.pallas_call(functools.partial(scoped_body, n, m, groups), out_shape=pl...  18.5 us
    unnamed x1, local copies, waits for them, and re-layouts  0.71 us

profile of v7, /device:TPU:17, one launch (start us, length us, event | category | flops | bytes accessed | tf_op | source)
XLA Modules:
  0.0 19.2 jit_solution(13319403569505341262)
XLA Ops:
  0.0 18.5 %shard_map.127 = f32[128,512]{1,0:T(8,128)S(1)} custom-call(f32[128,512]{1,0:T(8,128)} %args_0_.4, f32[1024,512]{1,0:T(8,128)} %args_1_.4, f32[1024,512]{1,0:T(8,128)} %args_2_.4, f32[512,1024]{1,0:T(8,128)} %args_3_.4, f32[16,128]{1,0:T(8,128)} %constant.4.clone.args_4_, bf16[4,256,256]{2,1,0:T(8,128)(2,1)} %constant.5.clone.args_5_, s32[1,32]{1,0:T(1,128)} %bitcast.5, ...), custom_call_target="tpu_custom_call" | custom-call | tf_op jit(solution)/shard_map/pallas_call | solution.py:456
  18.5 0.7 %copy.15 = f32[128,512]{1,0:T(8,128)} copy(f32[128,512]{1,0:T(8,128)S(1)} %shard_map.127) | data formatting | bytes 524288
